TPU v7x, 32 devices: a whole 2x2x4 slice. The times are simulated.
32 devices in a mesh: row: 4 (over z), col: 8 (over y, x, core).
Axes of the slice: x: 2, y: 2, z: 4, core: 2. Of those that a mesh axis runs over, the one named last changes fastest.
Arguments:
- points_rhs: bfloat16 [262144, 16], P(('row', 'col')), may hold values from -6 to 6
- leaf_basis: bfloat16 [1024, 256, 64], P(('row', 'col')), may hold values from -0.375 to 0.375
- near_src: int32 [1024, 2], P(('row', 'col')), may hold values from -1 to 1023, as said below
- near_blocks: bfloat16 [1024, 2, 256, 256], P(('row', 'col')), may hold values from -0.25 to 0.25
- transfer_first: bfloat16 [1024, 64, 64], P(('row', 'col')), may hold values from -0.5 to 0.5
- transfer_second: bfloat16 [512, 64, 64], P(('row', 'col')), may hold values from -0.5 to 0.5
- transfer_third: bfloat16 [256, 64, 64], P(('row', 'col')), may hold values from -0.5 to 0.5
- far_zero: int32 [1024, 8], P(('row', 'col')), may hold values from -1 to 1023, as said below
- far_one: int32 [512, 8], P(('row', 'col')), may hold values from -1 to 511, as said below
- far_two: int32 [256, 8], P(('row', 'col')), may hold values from -1 to 255, as said below
- far_three: int32 [128, 8], P(('row', 'col')), may hold values from -1 to 127, as said below
- couple_zero: bfloat16 [1024, 8, 64, 64], P(('row', 'col')), may hold values from -0.25 to 0.25
- couple_one: bfloat16 [512, 8, 64, 64], P(('row', 'col')), may hold values from -0.25 to 0.25
- couple_two: bfloat16 [256, 8, 64, 64], P(('row', 'col')), may hold values from -0.25 to 0.25
- couple_three: bfloat16 [128, 8, 64, 64], P(('row', 'col')), may hold values from -0.25 to 0.25
Outputs:
- product: bfloat16 [262144, 16], P(('row', 'col'))
Inputs may be any that keep to these rules, and one draw needn't show every extreme that they name: `near_src`: each entry is -1 or a leaf whose index differs from its row's by at most 2; -1 only where that leaf would lie outside the grid. `far_zero`: each row has 7 or 8 live entries, first in the row; a live entry of leaf i lies in the same aligned block of 256 leaves as i. `far_one`: each row has 7 or 8 live entries, first in the row; a live entry of cluster i lies in the same aligned block of 128 clusters as i. `far_two`: each row has 7 or 8 live entries, first in the row; a live entry of cluster i lies in the same aligned block of 64 clusters as i. `far_three`: each row has 7 or 8 live entries, first in the row; live entries may name any cluster of the level.
All inputs are finite; a program needn't handle non-finite values.
Results may differ from a plain program's by a relative error of at most 0.0044.
Values may be sent and summed in bfloat16 or wider, within the bound.
No kernel may reach another device: no remote copies, remote signals or barrier semaphores. Data moves between devices by JAX's collectives and lax.ppermute only.
A program may use at most 128 MiB of HBM per device.

v0:
```python
import jax
import jax.numpy as jnp
from jax import lax
from jax.sharding import PartitionSpec as P

LEAF = 256
RANK = 64
NRHS = 16
TOP_LEVEL = lax.Precision.HIGHEST


def padded_2(cells, sides, width):
    for axis, dim in sides:
        count = lax.axis_size(axis)
        ends = count - 1
        head = lax.slice_in_dim(cells, 0, width, axis=dim)
        tail = lax.slice_in_dim(cells, cells.shape[dim] - width, cells.shape[dim], axis=dim)
        cells = jnp.concatenate(
            [
                lax.ppermute(tail, axis, [(i, (i + 1) % count) for i in range(ends)]),
                cells,
                lax.ppermute(head, axis, [((i + 1) % count, i) for i in range(ends)]),
            ],
            axis=dim,
        )
    return cells


def gather_active(table, local_ids, sources):
    is_live = sources >= 0
    selected_rows = jnp.take(table, jnp.clip(local_ids, 0, table.shape[0] - 1), axis=0)
    return jnp.where(is_live[:, :, None, None], selected_rows, jnp.zeros_like(selected_rows))


def couple_level(table, group_start, sources, coupling_block):
    selected_rows = gather_active(table, sources - group_start, sources)
    return jnp.einsum(
        "enyd,endc->eyc", coupling_block, selected_rows, preferred_element_type=jnp.float32
    )


def collect_group(skeleton):
    return lax.all_gather(skeleton, "col", axis=0, tiled=True)


def shards(
    points_rhs,
    leaf_basis,
    near_src,
    near_blocks,
    transfer_first,
    transfer_second,
    transfer_third,
    far_zero,
    far_one,
    far_two,
    far_three,
    couple_zero,
    couple_one,
    couple_two,
    couple_three,
):
    leaf_count = leaf_basis.shape[0]
    leaf_x = points_rhs.reshape(leaf_count, LEAF, NRHS)
    padded = padded_2(points_rhs.reshape(leaf_count, LEAF * NRHS), ((("row", "col"), 0),), 2)
    padded = padded.reshape(leaf_count + 4, LEAF, NRHS)
    skel_zero = jnp.einsum(
        "lpa,lpr->lar", leaf_basis, leaf_x, preferred_element_type=jnp.float32
    ).astype(jnp.bfloat16)
    skeletons = [skel_zero]
    transfers = [transfer_first, transfer_second, transfer_third]
    for transfer in transfers:
        child_skel = skeletons[-1]
        lifted = jnp.einsum(
            "cab,car->cbr", transfer, child_skel, preferred_element_type=jnp.float32
        )
        lifted = lifted.reshape(lifted.shape[0] // 2, 2, RANK, NRHS).sum(axis=1)
        skeletons.append(lifted.astype(jnp.bfloat16))
    tables = [collect_group(skeletons[level_index]) for level_index in range(3)]
    coarse_group = lax.all_gather(skeletons[3], "col", axis=0, tiled=True)
    coarse_table = lax.all_gather(coarse_group, "row", axis=0, tiled=True)
    row_index = lax.axis_index("row")
    lists = [far_zero, far_one, far_two]
    coupling_blocks = [couple_zero, couple_one, couple_two]
    coupled_field = []
    for level_index in range(3):
        group_start = row_index * tables[level_index].shape[0]
        coupled_field.append(
            couple_level(
                tables[level_index], group_start, lists[level_index], coupling_blocks[level_index]
            )
        )
    coupled_field.append(couple_level(coarse_table, 0, far_three, couple_three))
    downward_field = coupled_field[3]
    for level_index in (3, 2, 1):
        spread = jnp.repeat(downward_field, 2, axis=0)
        downward_field = coupled_field[level_index - 1] + jnp.einsum(
            "cab,cbr->car",
            transfers[level_index - 1].astype(jnp.float32),
            spread,
            precision=TOP_LEVEL,
        )
    far_out = jnp.einsum(
        "lpa,lar->lpr", leaf_basis.astype(jnp.float32), downward_field, precision=TOP_LEVEL
    )
    first_leaf = lax.axis_index(("row", "col")) * leaf_count
    near_picked = gather_active(padded, near_src - first_leaf + 2, near_src)
    near_out = jnp.einsum(
        "iknm,ikmr->inr", near_blocks, near_picked, preferred_element_type=jnp.float32
    )
    return (far_out + near_out).reshape(leaf_count * LEAF, NRHS).astype(jnp.bfloat16)


def solution(mesh):
    return jax.shard_map(
        shards,
        mesh=mesh,
        in_specs=(
            P(("row", "col"), None),
            P(("row", "col"), None, None),
            P(("row", "col"), None),
            P(("row", "col"), None, None, None),
            P(("row", "col"), None, None),
            P(("row", "col"), None, None),
            P(("row", "col"), None, None),
            P(("row", "col"), None),
            P(("row", "col"), None),
            P(("row", "col"), None),
            P(("row", "col"), None),
            P(("row", "col"), None, None, None),
            P(("row", "col"), None, None, None),
            P(("row", "col"), None, None, None),
            P(("row", "col"), None, None, None),
        ),
        out_specs=P(("row", "col"), None),
        check_vma=False,
    )
```

profile of v0, /device:TPU:0, one launch (start us, length us, event | category | flops | bytes accessed | tf_op | source)
XLA Modules:
  0.0 106.1 jit_solution(7011895499649475544)
XLA Ops:
  0.0 0.9 fusion.44
  0.9 0.1 copy.67
  1.0 0.8 slice.13
  1.8 3.0 %collective-permute-start = (bf16[2,4096]{1,0:T(2,128)(2,1)}, bf16[2,4096]{1,0:T(2,128)(2,1)}, u32[]{:S(2)}, u32[]{:S(2)}) collective-permute-start(bf16[2,4096]{1,0:T(2,128)(2,1)} %slice.13), channel_id=1, source_target_pairs={{0,1},{1,2},{2,3},{3,4},{4,5},{5,6},{6,7},{7,8},{8,9},{9,10},{10,1... | collective-permute-start | bytes 49160 | tf_op jit(solution)/shard_map/ppermute | solution.py:20
  4.8 0.1 copy.68
  4.9 0.8 slice.15
  5.7 1.3 %collective-permute-start.1 = (bf16[2,4096]{1,0:T(2,128)(2,1)}, bf16[2,4096]{1,0:T(2,128)(2,1)}, u32[]{:S(2)}, u32[]{:S(2)}) collective-permute-start(bf16[2,4096]{1,0:T(2,128)(2,1)} %slice.15), channel_id=1, source_target_pairs={{1,0},{2,1},{3,2},{4,3},{5,4},{6,5},{7,6},{8,7},{9,8},{10,9},{11,1... | collective-permute-start | bytes 49160 | tf_op jit(solution)/shard_map/ppermute | solution.py:22
  7.0 0.7 compare_select_fusion.3
  7.7 1.3 %broadcast_compare_fusion.3 = (pred[4,8]{1,0:T(4,128)(4,1)}, pred[4,8]{1,0:T(4,128)(4,1)}) fusion(s32[4,8]{1,0:T(4,128)} %param.25), kind=kLoop, calls=%fused_computation.72 | loop fusion | flops 256 | bytes 192 | tf_op jit(solution)/shard_map/ge | solution.py:30
  8.9 1.3 %compare_and_fusion = (pred[8,8]{1,0:T(8,128)(4,1)}, s32[8,8]{1,0:T(8,128)S(1)}, pred[8,8]{1,0:T(8,128)(4,1)}) fusion(s32[8,8]{1,0:T(8,128)} %param.24, s32[]{:T(128)S(6)} %mul.17), kind=kLoop, calls=%fused_computation.64 | loop fusion | flops 576 | bytes 644 | tf_op jit(solution)/shard_map/jit(_take)/and | solution.py:31
  10.3 1.6 %convolution_convert_fusion = bf16[32,64,16]{1,2,0:T(8,128)(2,1)S(1)} fusion(bf16[32,256,64]{1,2,0:T(8,128)(2,1)} %param.16, bf16[2,32,8,256]{3,2,1,0:T(8,128)(2,1)} %bitcast.75), kind=kOutput, calls=%fused_computation.11 | convolution fusion | flops 16809984 | bytes 1376256 | tf_op jit(solution)/shard_map/lpa,lpr->lar/dot_general | solution.py:67
  11.9 14.6 %all_gather.15 = bf16[256,64,16]{1,2,0:T(8,128)(2,1)S(1)} all-gather(bf16[32,64,16]{1,2,0:T(8,128)(2,1)S(1)} %convolution_convert_fusion), channel_id=1, replica_groups=mesh['row'=4,'col'=8] {'col'}, dimensions={0}, use_global_device_ids=true | all-gather | bytes 589824 | tf_op jit(solution)/shard_map/all_gather | solution.py:43
  26.6 1.3 %bitcast_reduce_fusion = bf16[16,64,16]{1,2,0:T(8,128)(2,1)S(1)} fusion(bf16[32,64,16]{1,2,0:T(8,128)(2,1)S(1)} %convolution_convert_fusion, bf16[32,64,64]{2,1,0:T(8,128)(2,1)} %param.19), kind=kOutput, calls=%fused_computation.35 | convolution fusion | flops 4210688 | bytes 360448 | tf_op jit(solution)/shard_map/cab,car->cbr/dot_general | solution.py:74
  27.9 10.0 %all_gather.16 = bf16[128,64,16]{1,2,0:T(8,128)(2,1)} all-gather(bf16[16,64,16]{1,2,0:T(8,128)(2,1)S(1)} %bitcast_reduce_fusion), channel_id=1, replica_groups=mesh['row'=4,'col'=8] {'col'}, dimensions={0}, use_global_device_ids=true | all-gather | bytes 294912 | tf_op jit(solution)/shard_map/all_gather | solution.py:43
  37.8 0.2 bitcast_reduce_fusion.1
  38.0 9.2 %all_gather.17 = bf16[64,64,16]{1,2,0:T(8,128)(2,1)S(1)} all-gather(bf16[8,64,16]{1,2,0:T(8,128)(2,1)S(1)} %bitcast_reduce_fusion.1), channel_id=1, replica_groups=mesh['row'=4,'col'=8] {'col'}, dimensions={0}, use_global_device_ids=true | all-gather | bytes 147456 | tf_op jit(solution)/shard_map/all_gather | solution.py:43
  47.2 0.1 bitcast_reduce_fusion.2
  47.4 8.3 %all_gather.18 = bf16[32,64,16]{1,2,0:T(8,128)(2,1)S(1)} all-gather(bf16[4,64,16]{1,2,0:T(8,128)(2,1)S(1)} %bitcast_reduce_fusion.2), channel_id=1, replica_groups=mesh['row'=4,'col'=8] {'col'}, dimensions={0}, use_global_device_ids=true | all-gather | bytes 73728 | tf_op jit(solution)/shard_map/all_gather | solution.py:80
  55.7 17.5 %all_gather.19 = bf16[128,64,16]{1,2,0:T(8,128)(2,1)} all-gather(bf16[32,64,16]{1,2,0:T(8,128)(2,1)S(1)} %all_gather.18), channel_id=1, replica_groups=mesh['row'=4,'col'=8] {'row'}, dimensions={0}, use_global_device_ids=true | all-gather | bytes 327680 | tf_op jit(solution)/shard_map/all_gather | solution.py:81
  73.2 0.1 reshape.94
  73.4 0.1 reshape.78
  73.5 0.7 copy.62
  74.1 0.7 copy.63
  74.9 0.1 reshape.70
  75.0 0.1 copy.58
  75.1 0.7 copy.59
  75.8 1.3 %compare_and_fusion.3 = (pred[32,2]{0,1:T(4,128)(4,1)}, s32[32,2]{0,1:T(2,128)S(1)}, pred[32,2]{0,1:T(4,128)(4,1)}) fusion(s32[32,2]{0,1:T(2,128)} %param.17, s32[]{:T(128)S(6)} %mul.19), kind=kLoop, calls=%fused_computation.70 | loop fusion | flops 640 | bytes 644 | tf_op jit(solution)/shard_map/jit(_take)/and | solution.py:31
  77.0 0.1 copy.72
  77.1 0.7 reshape.102
  77.8 1.3 %gather_fusion.2 = bf16[64,64,16]{1,2,0:T(8,128)(2,1)} fusion(bf16[64,64,16]{1,2,0:T(8,128)(2,1)S(1)} %all_gather.17, s32[1024]{0:T(1024)S(1)} %pad_clamp_fusion.2), kind=kCustom, calls=%fused_computation.2 | custom fusion | bytes 262400 | tf_op jit(solution)/shard_map/jit(_take)/gather | solution.py:31
  79.1 1.6 %gather_fusion.3 = bf16[32,64,16]{1,2,0:T(8,128)(2,1)S(1)} fusion(bf16[128,64,16]{1,2,0:T(8,128)(2,1)} %all_gather.19, s32[1024]{0:T(1024)S(1)} %pad_clamp_fusion.1), kind=kCustom, calls=%fused_computation.3 | custom fusion | bytes 131200 | tf_op jit(solution)/shard_map/jit(_take)/gather | solution.py:31
  80.8 1.8 %convolution_bitcast_fusion.3 = f32[8,16,64]{2,1,0:T(8,128)S(1)} fusion(bf16[8,8,64,64]{3,2,1,0:T(8,128)(2,1)} %param.28, bf16[8,8,64,16]{2,3,1,0:T(8,128)(2,1)} %bitcast.73, pred[8,8]{1,0:T(8,128)(4,1)} %get-tuple-element.5, pred[8,8]{1,0:T(8,128)(4,1)} %get-tuple-element.15), kind=kOutput, calls=%fused_computation.17 | convolution fusion | flops 8519680 | bytes 688256 | tf_op jit(solution)/shard_map/enyd,endc->eyc/dot_general | solution.py:37
  82.5 1.4 %convolution_bitcast_fusion.4 = f32[4,64,16]{1,2,0:T(8,128)S(1)} fusion(bf16[4,8,64,64]{3,2,1,0:T(8,128)(2,1)} %param.29, bf16[4,8,64,16]{2,3,1,0:T(8,128)(2,1)S(1)} %bitcast.74, pred[4,8]{1,0:T(4,128)(4,1)} %get-tuple-element.19, pred[4,8]{1,0:T(4,128)(4,1)} %get-tuple-element.18), kind=kOutput, calls=%fused_computation.18 | convolution fusion | flops 4259840 | bytes 344128 | tf_op jit(solution)/shard_map/enyd,endc->eyc/dot_general | solution.py:37
  84.0 1.2 %fusion.3 = f32[8,64,16]{1,2,0:T(8,128)S(1)} fusion(f32[8,16,64]{2,1,0:T(8,128)S(1)} %convolution_bitcast_fusion.3, f32[8,64,16]{1,2,0:T(8,128)S(1)} %bitcast.80, bf16[8,64,64]{2,1,0:T(8,128)(2,1)} %param.21), kind=kOutput, calls=%fused_computation.16 | convolution fusion | flops 6299648 | bytes 163840 | tf_op jit(solution)/shard_map/cab,cbr->car/dot_general | solution.py:97
  85.2 2.5 %gather_fusion.1 = bf16[128,64,16]{1,2,0:T(8,128)(2,1)} fusion(bf16[128,64,16]{1,2,0:T(8,128)(2,1)} %all_gather.16, s32[1024]{0:T(1024)S(1)} %pad_clamp_fusion.3), kind=kCustom, calls=%fused_computation.1 | custom fusion | bytes 524800 | tf_op jit(solution)/shard_map/jit(_take)/gather | solution.py:31
  87.7 1.8 %convolution_bitcast_fusion.2 = f32[16,16,64]{2,1,0:T(8,128)S(1)} fusion(bf16[16,8,64,64]{3,2,1,0:T(8,128)(2,1)S(1)} %copy-done, bf16[16,8,64,16]{2,3,1,0:T(8,128)(2,1)} %bitcast.72, pred[16,8]{1,0:T(8,128)(4,1)} %copy.63, pred[16,8]{1,0:T(8,128)(4,1)S(1)} %copy-done.13), kind=kOutput, calls=%fused_computation.14 | convolution fusion | flops 17039360 | bytes 1376512 | tf_op jit(solution)/shard_map/enyd,endc->eyc/dot_general | solution.py:37
  89.5 0.5 fusion.2
  90.0 1.8 %gather_fusion = bf16[256,64,16]{1,2,0:T(8,128)(2,1)} fusion(bf16[256,64,16]{1,2,0:T(8,128)(2,1)S(1)} %all_gather.15, s32[1024]{0:T(1024)S(1)} %pad_clamp_fusion.4), kind=kCustom, calls=%fused_computation | custom fusion | bytes 1049600 | tf_op jit(solution)/shard_map/jit(_take)/gather | solution.py:31
  91.8 3.3 %convolution_bitcast_fusion.1 = f32[32,16,64]{2,1,0:T(8,128)S(1)} fusion(bf16[32,8,64,64]{3,2,1,0:T(8,128)(2,1)} %param.26, bf16[32,8,64,16]{2,3,1,0:T(8,128)(2,1)} %bitcast.71, pred[32,8]{1,0:T(8,128)(4,1)S(1)} %copy-done.7, pred[32,8]{1,0:T(8,128)(4,1)S(1)} %copy.58), kind=kOutput, calls=%fused_computation.9 | convolution fusion | flops 34078720 | bytes 2753024 | tf_op jit(solution)/shard_map/enyd,endc->eyc/dot_general | solution.py:37
  95.2 0.9 convolution_add_fusion.1
  96.2 0.1 copy.65
  96.3 0.1 copy.66
  96.4 0.9 concatenate.8
  97.4 0.9 concatenate.9
  98.4 0.6 gather_fusion.4
  99.0 5.8 %convolution_bitcast_fusion = f32[32,16,256]{2,1,0:T(8,128)S(1)} fusion(bf16[32,2,256,256]{3,2,1,0:T(8,128)(2,1)} %param.18, bf16[32,2,256,16]{2,3,1,0:T(8,128)(2,1)S(1)} %bitcast.70, pred[32,2]{1,0:T(8,128)(4,1)S(1)} %copy.66, pred[32,2]{1,0:T(8,128)(4,1)S(1)} %copy.65), kind=kOutput, calls=%fused_computation.6 | convolution fusion | flops 134742016 | bytes 9437312 | tf_op jit(solution)/shard_map/iknm,ikmr->inr/dot_general | solution.py:108
  104.8 0.6 fusion.1
  105.4 0.7 copy.80
  (47 shorter events, 0.6 us)
Async XLA Ops:
  0.0 87.7 %copy-start = (bf16[16,8,64,64]{3,2,1,0:T(8,128)(2,1)S(1)}, bf16[16,8,64,64]{3,2,1,0:T(8,128)(2,1)}, u32[]{:S(2)}) copy-start(bf16[16,8,64,64]{3,2,1,0:T(8,128)(2,1)} %param.27) | copy-start | bytes 3145732
  0.0 37.8 %copy-start.4 = (bf16[16,64,64]{2,1,0:T(8,128)(2,1)S(1)}, bf16[16,64,64]{2,1,0:T(8,128)(2,1)}, u32[]{:S(2)}) copy-start(bf16[16,64,64]{2,1,0:T(8,128)(2,1)} %param.20) | copy-start | bytes 393220
  0.0 47.2 %copy-start.6 = (bf16[8,64,64]{2,1,0:T(8,128)(2,1)S(1)}, bf16[8,64,64]{2,1,0:T(8,128)(2,1)}, u32[]{:S(2)}) copy-start(bf16[8,64,64]{2,1,0:T(8,128)(2,1)} %param.21) | copy-start | bytes 196612
  0.0 73.3 %copy-start.8 = (s32[16,8]{0,1:T(8,128)S(1)}, s32[16,8]{0,1:T(8,128)}, u32[]{:S(2)}) copy-start(s32[16,8]{0,1:T(8,128)} %param.23) | copy-start | bytes 1540
  0.0 74.8 %copy-start.9 = (s32[32,8]{0,1:T(8,128)S(1)}, s32[32,8]{0,1:T(8,128)}, u32[]{:S(2)}) copy-start(s32[32,8]{0,1:T(8,128)} %param.22) | copy-start | bytes 3076
  1.8 94.6 %collective-permute-start = (bf16[2,4096]{1,0:T(2,128)(2,1)}, bf16[2,4096]{1,0:T(2,128)(2,1)}, u32[]{:S(2)}, u32[]{:S(2)}) collective-permute-start(bf16[2,4096]{1,0:T(2,128)(2,1)} %slice.13), channel_id=1, source_target_pairs={{0,1},{1,2},{2,3},{3,4},{4,5},{5,6},{6,7},{7,8},{8,9},{9,10},{10,1... | collective-permute-start | bytes 49160 | tf_op jit(solution)/shard_map/ppermute | solution.py:20
  5.7 91.7 %collective-permute-start.1 = (bf16[2,4096]{1,0:T(2,128)(2,1)}, bf16[2,4096]{1,0:T(2,128)(2,1)}, u32[]{:S(2)}, u32[]{:S(2)}) collective-permute-start(bf16[2,4096]{1,0:T(2,128)(2,1)} %slice.15), channel_id=1, source_target_pairs={{1,0},{2,1},{3,2},{4,3},{5,4},{6,5},{7,6},{8,7},{9,8},{10,9},{11,1... | collective-permute-start | bytes 49160 | tf_op jit(solution)/shard_map/ppermute | solution.py:22
  79.1 8.6 %copy-start.13 = (pred[16,8]{1,0:T(8,128)(4,1)S(1)}, pred[16,8]{1,0:T(8,128)(4,1)}, u32[]{:S(2)}) copy-start(pred[16,8]{1,0:T(8,128)(4,1)} %copy.62) | copy-start | bytes 388
  82.5 7.0 %copy-start.5 = (bf16[16,64,64]{2,1,0:T(8,128)(2,1)S(1)}, bf16[16,64,64]{2,1,0:T(8,128)(2,1)}, u32[]{:S(2)}) copy-start(bf16[16,64,64]{2,1,0:T(8,128)(2,1)} %param.20) | copy-start | bytes 393220
  90.0 1.8 %copy-start.7 = (pred[32,8]{1,0:T(8,128)(4,1)S(1)}, pred[32,8]{1,0:T(8,128)(4,1)}, u32[]{:S(2)}) copy-start(pred[32,8]{1,0:T(8,128)(4,1)} %copy.59) | copy-start | bytes 772
  91.8 3.4 %copy-start.2 = (bf16[32,64,64]{2,1,0:T(8,128)(2,1)S(1)}, bf16[32,64,64]{2,1,0:T(8,128)(2,1)}, u32[]{:S(2)}) copy-start(bf16[32,64,64]{2,1,0:T(8,128)(2,1)} %param.19) | copy-start | bytes 786436
  91.8 4.4 %copy-start.12 = (s32[64]{0:T(128)S(1)}, s32[64]{0:T(128)}, u32[]{:S(2)}) copy-start(s32[64]{0:T(128)} %reshape.102) | copy-start | bytes 772
  91.8 4.4 %copy-start.3 = (bf16[8192,16]{0,1:T(8,128)(2,1)S(1)}, bf16[8192,16]{0,1:T(8,128)(2,1)}, u32[]{:S(2)}) copy-start(bf16[8192,16]{0,1:T(8,128)(2,1)} %param.15) | copy-start | bytes 786436
  91.8 4.4 %copy-start.11 = (pred[32,2]{0,1:T(4,128)(4,1)S(1)}, pred[32,2]{0,1:T(4,128)(4,1)}, u32[]{:S(2)}) copy-start(pred[32,2]{0,1:T(4,128)(4,1)} %get-tuple-element.20) | copy-start | bytes 196
  91.8 4.5 %copy-start.10 = (pred[32,2]{0,1:T(4,128)(4,1)S(1)}, pred[32,2]{0,1:T(4,128)(4,1)}, u32[]{:S(2)}) copy-start(pred[32,2]{0,1:T(4,128)(4,1)} %get-tuple-element.11) | copy-start | bytes 196
  99.0 5.8 %copy-start.1 = (bf16[32,256,64]{1,2,0:T(8,128)(2,1)S(1)}, bf16[32,256,64]{1,2,0:T(8,128)(2,1)}, u32[]{:S(2)}) copy-start(bf16[32,256,64]{1,2,0:T(8,128)(2,1)} %param.16) | copy-start | bytes 3145732
where the time goes:
time: 107 us; the launch traced here: 106 us
  blocking collectives  59.6 us (56%)
  matrix products  20.5 us (19%)
  local copies, waits for them, and re-layouts  16.8 us (16%)
  other arithmetic  4.61 us (4%)
  starting transfers between devices  4.27 us (4%)
    all_gather x3, blocking collectives, collect_group(): return lax.all_gather(skeleton, 'col', axis=0, tiled=True)  33.8 us
    all_gather x1, blocking collectives, shards(): coarse_table = lax.all_gather(coarse_group, 'row', axis=0, tiled=True)  17.5 us
    all_gather x1, blocking collectives, shards(): coarse_group = lax.all_gather(skeletons[3], 'col', axis=0, tiled=True)  8.34 us
    dot_general x4, matrix products, couple_level(): jnp.einsum('enyd,endc->eyc', coupling_block, selected_rows, preferred_ele...  8.29 us
    gather x5, local copies, waits for them, and re-layouts, gather_active(): jnp.take(table, jnp.clip(local_ids, 0, table.shape[0] - 1), axis=0)  7.86 us
    dot_general x1, matrix products, shards(): jnp.einsum('iknm,ikmr->inr', near_blocks, near_picked, preferred_element_...  5.76 us
    ppermute x1, starting transfers between devices, padded_2(): lax.ppermute(tail, axis, [(i, (i + 1) % count) for i in range(ends)])  2.99 us
    dot_general x3, matrix products, shards(): jnp.einsum('cab,cbr->car', transfers[level_index - 1].astype(jnp.float32)...  2.64 us
  transfers between devices with their start and end apart: 2, of which 0 were waited for; matrix products, arithmetic and copies ran while one was open for 30% of the time, Pallas kernels for 0%

commit v1 on v0

--- a/solution.py
+++ b/solution.py
@@ -78,7 +78,12 @@
         skeletons.append(lifted.astype(jnp.bfloat16))
     tables = [collect_group(skeletons[level_index]) for level_index in range(3)]
     coarse_group = lax.all_gather(skeletons[3], "col", axis=0, tiled=True)
-    coarse_table = lax.all_gather(coarse_group, "row", axis=0, tiled=True)
+    ring = [coarse_group]
+    for hop in range(3):
+        ring.append(lax.ppermute(ring[-1], "row", [(dev, (dev + 1) % 4) for dev in range(4)]))
+    coarse_table = jnp.roll(
+        jnp.concatenate(ring[::-1], axis=0), (lax.axis_index("row") + 1) * ring[0].shape[0], axis=0
+    )
     row_index = lax.axis_index("row")
     lists = [far_zero, far_one, far_two]
     coupling_blocks = [couple_zero, couple_one, couple_two]

time: 107 us -> 119 us (1.11)
  blocking collectives: 59.6 us -> 43.6 us
  local copies, waits for them, and re-layouts: 16.8 us -> 24.5 us
  matrix products: 20.5 us -> 28.1 us
  waiting for transfers between devices: 0.01 us -> 4.68 us
  starting transfers between devices: 4.27 us -> 8.58 us
  other arithmetic: 4.61 us -> 8.13 us
    all_gather x1 -> x0, blocking collectives: 17.5 us -> none  [shards(): coarse_table = lax.all_gather(coarse_group, 'row', axis=0, tiled=True)]
    ppermute x0 -> x3, starting transfers between devices: none -> 4.74 us  [shards(): lax.ppermute(ring[-1], 'row', [(dev, (dev + 1) % 4) for dev in range(4)])]
    ppermute x0 -> x3, waiting for transfers between devices: none -> 4.67 us  [shards(): lax.ppermute(ring[-1], 'row', [(dev, (dev + 1) % 4) for dev in range(4)])]
    gather x5, other arithmetic: 0.04 us -> 2.48 us  [gather_active(): jnp.take(table, jnp.clip(local_ids, 0, table.shape[0] - 1), axis=0)]
    all_gather x1, blocking collectives: 8.34 us -> 10.7 us  [shards(): coarse_group = lax.all_gather(skeletons[3], 'col', axis=0, tiled=True)]
    unnamed x28 -> x39, local copies, waits for them, and re-layouts: 0.06 us -> 2.1 us
    dot_general x3, matrix products: 2.64 us -> 4.66 us  [shards(): jnp.einsum('cab,cbr->car', transfers[level_index - 1].astype(jnp.float32)...]
    dot_general x3, matrix products: 1.63 us -> 3.54 us  [shards(): jnp.einsum('cab,car->cbr', transfer, child_skel, preferred_element_type=j...]
  transfers between devices with their start and end apart: 2 -> 5, of which waited for: 0 -> 1; matrix products, arithmetic and copies ran while one was open for 30% -> 36% of each run, Pallas kernels for 0% -> 0%
where the time goes in v1:
time: 119 us; the launch traced here: 118 us
  blocking collectives  43.6 us (37%)
  matrix products  28.1 us (24%)
  local copies, waits for them, and re-layouts  24.5 us (21%)
  starting transfers between devices  8.58 us (7%)
  other arithmetic  8.13 us (7%)
  waiting for transfers between devices  4.68 us (4%)
    all_gather x3, blocking collectives, collect_group(): return lax.all_gather(skeleton, 'col', axis=0, tiled=True)  32.9 us
    all_gather x1, blocking collectives, shards(): coarse_group = lax.all_gather(skeletons[3], 'col', axis=0, tiled=True)  10.7 us
    dot_general x4, matrix products, couple_level(): jnp.einsum('enyd,endc->eyc', coupling_block, selected_rows, preferred_ele...  9.98 us
    gather x5, local copies, waits for them, and re-layouts, gather_active(): jnp.take(table, jnp.clip(local_ids, 0, table.shape[0] - 1), axis=0)  8.1 us
    dot_general x1, matrix products, shards(): jnp.einsum('iknm,ikmr->inr', near_blocks, near_picked, preferred_element_...  6.49 us
    ppermute x3, starting transfers between devices, shards(): lax.ppermute(ring[-1], 'row', [(dev, (dev + 1) % 4) for dev in range(4)])  4.74 us
    ppermute x3, waiting for transfers between devices, shards(): lax.ppermute(ring[-1], 'row', [(dev, (dev + 1) % 4) for dev in range(4)])  4.67 us
    dot_general x3, matrix products, shards(): jnp.einsum('cab,cbr->car', transfers[level_index - 1].astype(jnp.float32)...  4.66 us
  transfers between devices with their start and end apart: 5, of which 1 were waited for; matrix products, arithmetic and copies ran while one was open for 36% of the time, Pallas kernels for 0%

profile of v1, /device:TPU:0, one launch (start us, length us, event | category | flops | bytes accessed | tf_op | source)
XLA Modules:
  0.0 117.9 jit_solution(16793975363139926753)
XLA Ops:
  0.0 1.8 %convolution_convert_fusion = bf16[32,64,16]{1,2,0:T(8,128)(2,1)S(1)} fusion(bf16[32,256,64]{1,2,0:T(8,128)(2,1)} %param.16, bf16[2,32,8,256]{3,2,1,0:T(8,128)(2,1)} %bitcast.75), kind=kOutput, calls=%fused_computation.11 | convolution fusion | flops 16809984 | bytes 1376256 | tf_op jit(solution)/shard_map/lpa,lpr->lar/dot_general | solution.py:67
  1.8 1.4 %bitcast_reduce_fusion = bf16[16,64,16]{1,2,0:T(8,128)(2,1)S(1)} fusion(bf16[32,64,16]{1,2,0:T(8,128)(2,1)S(1)} %convolution_convert_fusion, bf16[32,64,64]{2,1,0:T(8,128)(2,1)} %param.19), kind=kOutput, calls=%fused_computation.35 | convolution fusion | flops 4210688 | bytes 360448 | tf_op jit(solution)/shard_map/cab,car->cbr/dot_general | solution.py:74
  3.2 1.1 bitcast_reduce_fusion.1
  4.3 1.1 bitcast_reduce_fusion.2
  5.4 10.7 %all_gather.15 = bf16[32,64,16]{1,2,0:T(8,128)(2,1)S(1)} all-gather(bf16[4,64,16]{1,2,0:T(8,128)(2,1)S(1)} %bitcast_reduce_fusion.2), channel_id=1, replica_groups=mesh['row'=4,'col'=8] {'col'}, dimensions={0}, use_global_device_ids=true | all-gather | bytes 73728 | tf_op jit(solution)/shard_map/all_gather | solution.py:80
  16.1 1.6 %collective-permute-start = (bf16[32,64,16]{1,2,0:T(8,128)(2,1)S(1)}, bf16[32,64,16]{1,2,0:T(8,128)(2,1)}, u32[]{:S(2)}, u32[]{:S(2)}) collective-permute-start(bf16[32,64,16]{1,2,0:T(8,128)(2,1)S(1)} %all_gather.15), channel_id=1, source_target_pairs={{0,8},{8,16},{16,24},{24,0},{1,9},{9,17},{17,25},{25,1},{2,10},{10... | collective-permute-start | bytes 196616 | tf_op jit(solution)/shard_map/ppermute | solution.py:83
  17.7 0.7 fusion.44
  18.5 0.8 slice.13
  19.3 2.6 %collective-permute-start.3 = (bf16[2,4096]{1,0:T(2,128)(2,1)}, bf16[2,4096]{1,0:T(2,128)(2,1)}, u32[]{:S(2)}, u32[]{:S(2)}) collective-permute-start(bf16[2,4096]{1,0:T(2,128)(2,1)} %slice.13), channel_id=1, source_target_pairs={{0,1},{1,2},{2,3},{3,4},{4,5},{5,6},{6,7},{7,8},{8,9},{9,10},{10,1... | collective-permute-start | bytes 49160 | tf_op jit(solution)/shard_map/ppermute | solution.py:20
  22.0 0.8 slice.15
  22.7 1.3 %collective-permute-start.4 = (bf16[2,4096]{1,0:T(2,128)(2,1)}, bf16[2,4096]{1,0:T(2,128)(2,1)}, u32[]{:S(2)}, u32[]{:S(2)}) collective-permute-start(bf16[2,4096]{1,0:T(2,128)(2,1)} %slice.15), channel_id=1, source_target_pairs={{1,0},{2,1},{3,2},{4,3},{5,4},{6,5},{7,6},{8,7},{9,8},{10,9},{11,1... | collective-permute-start | bytes 49160 | tf_op jit(solution)/shard_map/ppermute | solution.py:22
  24.0 0.7 compare_select_fusion.3
  24.7 1.2 %broadcast_compare_fusion.3 = (pred[4,8]{1,0:T(4,128)(4,1)}, pred[4,8]{1,0:T(4,128)(4,1)}) fusion(s32[4,8]{1,0:T(4,128)} %param.25), kind=kLoop, calls=%fused_computation.80 | loop fusion | flops 256 | bytes 192 | tf_op jit(solution)/shard_map/ge | solution.py:30
  25.9 11.9 %all_gather.14 = bf16[64,64,16]{1,2,0:T(8,128)(2,1)S(1)} all-gather(bf16[8,64,16]{1,2,0:T(8,128)(2,1)S(1)} %bitcast_reduce_fusion.1), channel_id=1, replica_groups=mesh['row'=4,'col'=8] {'col'}, dimensions={0}, use_global_device_ids=true | all-gather | bytes 147456 | tf_op jit(solution)/shard_map/all_gather | solution.py:43
  37.8 9.9 %all_gather.13 = bf16[128,64,16]{1,2,0:T(8,128)(2,1)} all-gather(bf16[16,64,16]{1,2,0:T(8,128)(2,1)S(1)} %bitcast_reduce_fusion), channel_id=1, replica_groups=mesh['row'=4,'col'=8] {'col'}, dimensions={0}, use_global_device_ids=true | all-gather | bytes 294912 | tf_op jit(solution)/shard_map/all_gather | solution.py:43
  47.7 11.1 %all_gather.12 = bf16[256,64,16]{1,2,0:T(8,128)(2,1)S(1)} all-gather(bf16[32,64,16]{1,2,0:T(8,128)(2,1)} %copy-done.5), channel_id=1, replica_groups=mesh['row'=4,'col'=8] {'col'}, dimensions={0}, use_global_device_ids=true | all-gather | bytes 589824 | tf_op jit(solution)/shard_map/all_gather | solution.py:43
  62.1 1.3 %copy.62 = pred[16,8]{1,0:T(8,128)(4,1)} copy(pred[16,8]{0,1:T(8,128)(4,1)} %get-tuple-element.16) | data formatting | bytes 256 | tf_op jit(solution)/shard_map/ge | solution.py:30
  63.5 1.3 %copy.63 = pred[16,8]{1,0:T(8,128)(4,1)} copy(pred[16,8]{0,1:T(8,128)(4,1)} %get-tuple-element.7) | data formatting | bytes 256 | tf_op jit(solution)/shard_map/jit(_take)/and | solution.py:31
  64.8 1.3 %compare_and_fusion.2 = (pred[32,8]{0,1:T(8,128)(4,1)}, s32[32,8]{0,1:T(8,128)}, pred[32,8]{0,1:T(8,128)(4,1)}) fusion(s32[32,8]{0,1:T(8,128)} %param.22, s32[]{:T(128)S(6)} %mul.18), kind=kLoop, calls=%fused_computation.74 | loop fusion | flops 2304 | bytes 2564 | tf_op jit(solution)/shard_map/jit(_take)/and | solution.py:31
  66.1 0.8 copy.61
  67.5 0.7 pad_clamp_fusion.4
  68.2 0.8 copy.58
  69.0 0.8 copy.59
  69.7 1.2 %compare_and_fusion.3 = (pred[32,2]{0,1:T(4,128)(4,1)}, s32[32,2]{0,1:T(2,128)S(1)}, pred[32,2]{0,1:T(4,128)(4,1)}) fusion(s32[32,2]{0,1:T(2,128)} %param.17, s32[]{:T(128)S(6)} %mul.23), kind=kLoop, calls=%fused_computation.78 | loop fusion | flops 640 | bytes 644 | tf_op jit(solution)/shard_map/jit(_take)/and | solution.py:31
  70.9 0.7 copy.72
  71.6 1.4 %reshape.102 = s32[64]{0:T(128)} reshape(s32[32,2]{1,0:T(8,128)} %copy.72) | data formatting | bytes 512 | tf_op jit(solution)/shard_map/jit(_take)/broadcast_in_dim | solution.py:31
  73.1 1.4 %gather_fusion.2 = bf16[64,64,16]{1,2,0:T(8,128)(2,1)} fusion(bf16[64,64,16]{1,2,0:T(8,128)(2,1)S(1)} %all_gather.14, s32[1024]{0:T(1024)} %pad_clamp_fusion.2), kind=kCustom, calls=%fused_computation.2 | custom fusion | bytes 262400 | tf_op jit(solution)/shard_map/jit(_take)/gather | solution.py:31
  74.5 2.7 %gather_fusion.1 = bf16[128,64,16]{1,2,0:T(8,128)(2,1)} fusion(bf16[128,64,16]{1,2,0:T(8,128)(2,1)} %all_gather.13, s32[1024]{0:T(1024)} %pad_clamp_fusion.3), kind=kCustom, calls=%fused_computation.1 | custom fusion | bytes 524800 | tf_op jit(solution)/shard_map/jit(_take)/gather | solution.py:31
  77.2 1.8 %gather_fusion = bf16[256,64,16]{1,2,0:T(8,128)(2,1)} fusion(bf16[256,64,16]{1,2,0:T(8,128)(2,1)S(1)} %all_gather.12, s32[1024]{0:T(1024)S(1)} %pad_clamp_fusion.4), kind=kCustom, calls=%fused_computation | custom fusion | bytes 1049600 | tf_op jit(solution)/shard_map/jit(_take)/gather | solution.py:31
  78.9 2.4 %convolution_bitcast_fusion.3 = f32[8,16,64]{2,1,0:T(8,128)} fusion(bf16[8,8,64,64]{3,2,1,0:T(8,128)(2,1)} %param.28, bf16[8,8,64,16]{2,3,1,0:T(8,128)(2,1)S(1)} %bitcast.73, pred[8,8]{1,0:T(8,128)(4,1)S(1)} %copy-done.13, pred[8,8]{1,0:T(8,128)(4,1)} %get-tuple-element.15), kind=kOutput, calls=%fused_computation.17 | convolution fusion | flops 8519680 | bytes 688256 | tf_op jit(solution)/shard_map/enyd,endc->eyc/dot_general | solution.py:37
  81.4 2.5 %convolution_bitcast_fusion.2 = f32[16,16,64]{2,1,0:T(8,128)} fusion(bf16[16,8,64,64]{3,2,1,0:T(8,128)(2,1)S(1)} %copy-done, bf16[16,8,64,16]{2,3,1,0:T(8,128)(2,1)} %bitcast.72, pred[16,8]{1,0:T(8,128)(4,1)} %copy.63, pred[16,8]{1,0:T(8,128)(4,1)} %copy.62), kind=kOutput, calls=%fused_computation.14 | convolution fusion | flops 17039360 | bytes 1376512 | tf_op jit(solution)/shard_map/enyd,endc->eyc/dot_general | solution.py:37
  83.8 3.8 %convolution_bitcast_fusion.1 = f32[32,16,64]{2,1,0:T(8,128)} fusion(bf16[32,8,64,64]{3,2,1,0:T(8,128)(2,1)} %param.26, bf16[32,8,64,16]{2,3,1,0:T(8,128)(2,1)S(1)} %bitcast.71, pred[32,8]{1,0:T(8,128)(4,1)S(1)} %copy.59, pred[32,8]{1,0:T(8,128)(4,1)S(1)} %copy.58), kind=kOutput, calls=%fused_computation.9 | convolution fusion | flops 34078720 | bytes 2753024 | tf_op jit(solution)/shard_map/enyd,endc->eyc/dot_general | solution.py:37
  87.9 0.9 concatenate.15
  88.9 0.9 concatenate.16
  89.8 2.5 %collective-permute-start.1 = (bf16[32,64,16]{1,2,0:T(8,128)(2,1)}, bf16[32,64,16]{1,2,0:T(8,128)(2,1)S(1)}, u32[]{:S(2)}, u32[]{:S(2)}) collective-permute-start(bf16[32,64,16]{1,2,0:T(8,128)(2,1)} %collective-permute-done), channel_id=1, source_target_pairs={{0,8},{8,16},{16,24},{24,0},{1,9},{9,17},{17,25},{25,1},{2,10},{10... | collective-permute-start | bytes 196616 | tf_op jit(solution)/shard_map/ppermute | solution.py:83
  93.0 4.7 %collective-permute-done.1 = bf16[32,64,16]{1,2,0:T(8,128)(2,1)S(1)} collective-permute-done((bf16[32,64,16]{1,2,0:T(8,128)(2,1)}, bf16[32,64,16]{1,2,0:T(8,128)(2,1)S(1)}, u32[]{:S(2)}, u32[]{:S(2)}) %collective-permute-start.1) | collective-permute-done | bytes 65568 | tf_op jit(solution)/shard_map/ppermute | solution.py:83
  97.6 0.7 collective-permute-start.2
  98.3 6.5 %convolution_bitcast_fusion = f32[32,16,256]{2,1,0:T(8,128)} fusion(bf16[32,2,256,256]{3,2,1,0:T(8,128)(2,1)} %param.18, bf16[32,2,256,16]{2,3,1,0:T(8,128)(2,1)S(1)} %bitcast.70, pred[32,2]{1,0:T(8,128)(4,1)S(1)} %copy.66, pred[32,2]{1,0:T(8,128)(4,1)S(1)} %copy.65), kind=kOutput, calls=%fused_computation.6 | convolution fusion | flops 134742016 | bytes 9437312 | tf_op jit(solution)/shard_map/iknm,ikmr->inr/dot_general | solution.py:113
  104.9 1.0 constant_dynamic-update-slice_fusion.5
  106.0 0.9 constant_dynamic-update-slice_fusion.1
  106.9 0.8 constant_dynamic-slice_fusion
  107.8 1.6 %gather_fusion.3 = bf16[32,64,16]{1,2,0:T(8,128)(2,1)S(1)} fusion(bf16[128,64,16]{1,2,0:T(8,128)(2,1)} %constant_dynamic-slice_fusion, s32[1024]{0:T(1024)S(1)} %copy-done.7), kind=kCustom, calls=%fused_computation.3 | custom fusion | bytes 131200 | tf_op jit(solution)/shard_map/jit(_take)/gather | solution.py:31
  109.4 1.3 %convolution_bitcast_fusion.4 = f32[4,64,16]{1,2,0:T(8,128)S(1)} fusion(bf16[4,8,64,64]{3,2,1,0:T(8,128)(2,1)} %param.29, bf16[4,8,64,16]{2,3,1,0:T(8,128)(2,1)S(1)} %bitcast.74, pred[4,8]{1,0:T(4,128)(4,1)S(1)} %copy-done.15, pred[4,8]{1,0:T(4,128)(4,1)S(1)} %copy-done.14), kind=kOutput, calls=%fused_computation.18 | convolution fusion | flops 4259840 | bytes 344128 | tf_op jit(solution)/shard_map/enyd,endc->eyc/dot_general | solution.py:37
  110.8 1.1 fusion.3
  112.0 1.5 %fusion.2 = f32[16,64,16]{1,2,0:T(8,128)S(1)} fusion(f32[16,16,64]{2,1,0:T(8,128)} %convolution_bitcast_fusion.2, f32[16,64,16]{1,2,0:T(8,128)S(1)} %bitcast.79, bf16[16,64,64]{2,1,0:T(8,128)(2,1)} %param.20), kind=kOutput, calls=%fused_computation.13 | convolution fusion | flops 12599296 | bytes 327680 | tf_op jit(solution)/shard_map/cab,cbr->car/dot_general | solution.py:102
  113.5 2.0 %convolution_add_fusion.1 = f32[32,16,64]{2,1,0:T(8,128)S(1)} fusion(f32[32,16,64]{2,1,0:T(8,128)} %convolution_bitcast_fusion.1, f32[32,64,16]{1,2,0:T(8,128)S(1)} %bitcast.77, bf16[32,64,64]{2,1,0:T(8,128)(2,1)} %param.19), kind=kOutput, calls=%fused_computation.8 | convolution fusion | flops 25198592 | bytes 655360 | tf_op jit(solution)/shard_map/cab,cbr->car/dot_general | solution.py:102
  115.5 1.6 %fusion.1 = bf16[32,2,8,256]{3,2,1,0:T(8,128)(2,1)S(1)} fusion(f32[32,16,256]{2,1,0:T(8,128)} %convolution_bitcast_fusion, f32[32,16,64]{2,1,0:T(8,128)S(1)} %convolution_add_fusion.1, bf16[32,256,64]{1,2,0:T(8,128)(2,1)S(1)} %copy-done.2), kind=kOutput, calls=%fused_computation.10 | convolution fusion | flops 100925440 | bytes 1966080 | tf_op jit(solution)/shard_map/lpa,lar->lpr/dot_general | solution.py:108
  117.1 0.7 copy.80
  (65 shorter events, 5.5 us)
Async XLA Ops:
  0.0 81.3 %copy-start = (bf16[16,8,64,64]{3,2,1,0:T(8,128)(2,1)S(1)}, bf16[16,8,64,64]{3,2,1,0:T(8,128)(2,1)}, u32[]{:S(2)}) copy-start(bf16[16,8,64,64]{3,2,1,0:T(8,128)(2,1)} %param.27) | copy-start | bytes 3145732
  0.0 59.5 %copy-start.8 = (s32[8,8]{1,0:T(8,128)S(1)}, s32[8,8]{1,0:T(8,128)}, u32[]{:S(2)}) copy-start(s32[8,8]{1,0:T(8,128)} %param.24) | copy-start | bytes 772
  0.0 60.8 %copy-start.9 = (s32[16,8]{0,1:T(8,128)S(1)}, s32[16,8]{0,1:T(8,128)}, u32[]{:S(2)}) copy-start(s32[16,8]{0,1:T(8,128)} %param.23) | copy-start | bytes 1540
  1.8 3.6 %copy-start.5 = (bf16[32,64,16]{1,2,0:T(8,128)(2,1)}, bf16[32,64,16]{1,2,0:T(8,128)(2,1)S(1)}, u32[]{:S(2)}) copy-start(bf16[32,64,16]{1,2,0:T(8,128)(2,1)S(1)} %convolution_convert_fusion) | copy-start | bytes 196612
  16.1 73.7 %collective-permute-start = (bf16[32,64,16]{1,2,0:T(8,128)(2,1)S(1)}, bf16[32,64,16]{1,2,0:T(8,128)(2,1)}, u32[]{:S(2)}, u32[]{:S(2)}) collective-permute-start(bf16[32,64,16]{1,2,0:T(8,128)(2,1)S(1)} %all_gather.15), channel_id=1, source_target_pairs={{0,8},{8,16},{16,24},{24,0},{1,9},{9,17},{17,25},{25,1},{2,10},{10... | collective-permute-start | bytes 196616 | tf_op jit(solution)/shard_map/ppermute | solution.py:83
  19.3 68.6 %collective-permute-start.3 = (bf16[2,4096]{1,0:T(2,128)(2,1)}, bf16[2,4096]{1,0:T(2,128)(2,1)}, u32[]{:S(2)}, u32[]{:S(2)}) collective-permute-start(bf16[2,4096]{1,0:T(2,128)(2,1)} %slice.13), channel_id=1, source_target_pairs={{0,1},{1,2},{2,3},{3,4},{4,5},{5,6},{6,7},{7,8},{8,9},{9,10},{10,1... | collective-permute-start | bytes 49160 | tf_op jit(solution)/shard_map/ppermute | solution.py:20
  22.7 66.1 %collective-permute-start.4 = (bf16[2,4096]{1,0:T(2,128)(2,1)}, bf16[2,4096]{1,0:T(2,128)(2,1)}, u32[]{:S(2)}, u32[]{:S(2)}) collective-permute-start(bf16[2,4096]{1,0:T(2,128)(2,1)} %slice.15), channel_id=1, source_target_pairs={{1,0},{2,1},{3,2},{4,3},{5,4},{6,5},{7,6},{8,7},{9,8},{10,9},{11,1... | collective-permute-start | bytes 49160 | tf_op jit(solution)/shard_map/ppermute | solution.py:22
  77.2 1.8 %copy-start.3 = (bf16[64,64,16]{1,2,0:T(8,128)(2,1)S(1)}, bf16[64,64,16]{1,2,0:T(8,128)(2,1)}, u32[]{:S(2)}) copy-start(bf16[64,64,16]{1,2,0:T(8,128)(2,1)} %gather_fusion.2) | copy-start | bytes 393220
  77.2 1.8 %copy-start.13 = (pred[8,8]{1,0:T(8,128)(4,1)S(1)}, pred[8,8]{1,0:T(8,128)(4,1)}, u32[]{:S(2)}) copy-start(pred[8,8]{1,0:T(8,128)(4,1)} %get-tuple-element.5) | copy-start | bytes 196
  78.9 4.9 %copy-start.1 = (bf16[256,64,16]{1,2,0:T(8,128)(2,1)S(1)}, bf16[256,64,16]{1,2,0:T(8,128)(2,1)}, u32[]{:S(2)}) copy-start(bf16[256,64,16]{1,2,0:T(8,128)(2,1)} %gather_fusion) | copy-start | bytes 1572868
  81.3 6.3 %copy-start.12 = (s32[64]{0:T(128)S(1)}, s32[64]{0:T(128)}, u32[]{:S(2)}) copy-start(s32[64]{0:T(128)} %reshape.102) | copy-start | bytes 772
  81.3 6.3 %copy-start.4 = (bf16[8192,16]{0,1:T(8,128)(2,1)S(1)}, bf16[8192,16]{0,1:T(8,128)(2,1)}, u32[]{:S(2)}) copy-start(bf16[8192,16]{0,1:T(8,128)(2,1)} %param.15) | copy-start | bytes 786436
  81.4 6.3 %copy-start.11 = (pred[32,2]{0,1:T(4,128)(4,1)S(1)}, pred[32,2]{0,1:T(4,128)(4,1)}, u32[]{:S(2)}) copy-start(pred[32,2]{0,1:T(4,128)(4,1)} %get-tuple-element.20) | copy-start | bytes 196
  81.4 6.4 %copy-start.10 = (pred[32,2]{0,1:T(4,128)(4,1)S(1)}, pred[32,2]{0,1:T(4,128)(4,1)}, u32[]{:S(2)}) copy-start(pred[32,2]{0,1:T(4,128)(4,1)} %get-tuple-element.11) | copy-start | bytes 196
  89.8 7.8 %collective-permute-start.1 = (bf16[32,64,16]{1,2,0:T(8,128)(2,1)}, bf16[32,64,16]{1,2,0:T(8,128)(2,1)S(1)}, u32[]{:S(2)}, u32[]{:S(2)}) collective-permute-start(bf16[32,64,16]{1,2,0:T(8,128)(2,1)} %collective-permute-done), channel_id=1, source_target_pairs={{0,8},{8,16},{16,24},{24,0},{1,9},{9,17},{17,25},{25,1},{2,10},{10... | collective-permute-start | bytes 196616 | tf_op jit(solution)/shard_map/ppermute | solution.py:83
  97.6 7.2 %collective-permute-start.2 = (bf16[32,64,16]{1,2,0:T(8,128)(2,1)S(1)}, bf16[32,64,16]{1,2,0:T(8,128)(2,1)S(1)}, u32[]{:S(2)}, u32[]{:S(2)}) collective-permute-start(bf16[32,64,16]{1,2,0:T(8,128)(2,1)S(1)} %collective-permute-done.1), channel_id=1, source_target_pairs={{0,8},{8,16},{16,24},{24,0},{1,9},{9,17},{17,25},{25,1},{2,10},{10... | collective-permute-start | bytes 196616 | tf_op jit(solution)/shard_map/ppermute | solution.py:83
  98.3 9.5 %copy-start.7 = (s32[1024]{0:T(1024)S(1)}, s32[1024]{0:T(1024)}, u32[]{:S(2)}) copy-start(s32[1024]{0:T(1024)} %pad_clamp_fusion.1) | copy-start | bytes 12292
  104.8 4.6 %copy-start.14 = (pred[4,8]{1,0:T(4,128)(4,1)S(1)}, pred[4,8]{1,0:T(4,128)(4,1)}, u32[]{:S(2)}) copy-start(pred[4,8]{1,0:T(4,128)(4,1)} %get-tuple-element.18) | copy-start | bytes 100
  104.8 4.6 %copy-start.15 = (pred[4,8]{1,0:T(4,128)(4,1)S(1)}, pred[4,8]{1,0:T(4,128)(4,1)}, u32[]{:S(2)}) copy-start(pred[4,8]{1,0:T(4,128)(4,1)} %get-tuple-element.19) | copy-start | bytes 100
  104.8 6.0 %copy-start.6 = (bf16[8,64,64]{2,1,0:T(8,128)(2,1)S(1)}, bf16[8,64,64]{2,1,0:T(8,128)(2,1)}, u32[]{:S(2)}) copy-start(bf16[8,64,64]{2,1,0:T(8,128)(2,1)} %param.21) | copy-start | bytes 196612
  104.8 10.7 %copy-start.2 = (bf16[32,256,64]{1,2,0:T(8,128)(2,1)S(1)}, bf16[32,256,64]{1,2,0:T(8,128)(2,1)}, u32[]{:S(2)}) copy-start(bf16[32,256,64]{1,2,0:T(8,128)(2,1)} %param.16) | copy-start | bytes 3145732
